TPU v7x, 32 devices: a whole 2x2x4 slice. The times are simulated.
32 devices in a mesh: tm: 8 (over z, y), series: 4 (over x, core).
Axes of the slice: x: 2, y: 2, z: 4, core: 2. Of those that a mesh axis runs over, the one named last changes fastest.
Arguments:
- signal: float32 [64, 262144], P('series', 'tm')
- valid_start: int32 [64], replicated, may hold values from 0 to 65535
- valid_end: int32 [64], replicated, may hold values from 196609 to 262144
Outputs:
- smooth: float32 [64, 262144], P('series', 'tm')
- slope: float32 [64, 262144], P('series', 'tm')
- covariance: float32 [64, 64], P('series')
Inputs may be any that keep to these rules, and one draw needn't show every extreme that they name: `valid_end`: end of the valid samples of each series.
All inputs are finite; a program needn't handle non-finite values.
Results may differ from a plain program's by a relative error of at most 0.00015.
Values sent between devices are 32-bit elements; how exact they have to be, the bound alone decides.
A program may use at most 64 MiB of HBM per device.

v0:
```python
import jax
import jax.numpy as jnp
from jax import lax
from jax.sharding import PartitionSpec as P

HALF = 16


def padded(cells, sides, width):
    for axis, dim in sides:
        count = lax.axis_size(axis)
        ends = count - 1
        head = lax.slice_in_dim(cells, 0, width, axis=dim)
        tail = lax.slice_in_dim(cells, cells.shape[dim] - width, cells.shape[dim], axis=dim)
        cells = jnp.concatenate(
            [
                lax.ppermute(tail, axis, [(i, (i + 1) % count) for i in range(ends)]),
                cells,
                lax.ppermute(head, axis, [((i + 1) % count, i) for i in range(ends)]),
            ],
            axis=dim,
        )
    return cells


def cross_rows(left, right):
    return lax.dot_general(
        left,
        right,
        (((1,), (1,)), ((), ())),
        precision=lax.Precision.HIGHEST,
        preferred_element_type=jnp.float32,
    )


def held_value(field, spot):
    return jnp.take_along_axis(field, spot, axis=1)


def shards(signal, valid_start, valid_end):
    rows, width = signal.shape
    taps = 2 * HALF + 1
    offsets = jnp.arange(-HALF, HALF + 1).astype(jnp.float32)
    second = jnp.sum(offsets * offsets)
    centre_sq = second / taps
    curved = offsets * offsets - centre_sq
    fourth = jnp.sum(curved * curved)
    extended = padded(signal, (("tm", 1),), 2 * HALF)
    span = width + 2 * HALF
    level = jnp.zeros((rows, span), jnp.float32)
    tilt = jnp.zeros((rows, span), jnp.float32)
    bend = jnp.zeros((rows, span), jnp.float32)
    for m in range(taps):
        window = extended[:, m : m + span]
        level = level + window * (1.0 / taps)
        tilt = tilt + window * (offsets[m] / second)
        bend = bend + window * (curved[m] / fourth)
    begin = lax.axis_index("tm") * width
    group = lax.axis_index("series") * rows
    first = lax.dynamic_slice_in_dim(valid_start, group, rows)[:, None]
    last = lax.dynamic_slice_in_dim(valid_end, group, rows)[:, None]
    moment = begin + jnp.arange(width, dtype=jnp.int32)[None, :]
    low_centre = first + HALF
    high_centre = last - HALF - 1
    centre = jnp.clip(moment, low_centre, high_centre)
    low_spot = jnp.clip(low_centre - begin + HALF, 0, span - 1)
    high_spot = jnp.clip(high_centre - begin + HALF, 0, span - 1)
    below = moment < low_centre
    above = moment > high_centre
    along = (moment - centre).astype(jnp.float32)
    lv = jnp.where(
        below,
        held_value(level, low_spot),
        jnp.where(above, held_value(level, high_spot), level[:, HALF : HALF + width]),
    )
    tl = jnp.where(
        below,
        held_value(tilt, low_spot),
        jnp.where(above, held_value(tilt, high_spot), tilt[:, HALF : HALF + width]),
    )
    bd = jnp.where(
        below,
        held_value(bend, low_spot),
        jnp.where(above, held_value(bend, high_spot), bend[:, HALF : HALF + width]),
    )
    inside = (moment >= first) & (moment < last)
    smooth = jnp.where(inside, lv + tl * along + bd * (along * along - centre_sq), 0.0)
    slope = jnp.where(inside, HALF * (tl + 2.0 * along * bd), 0.0)
    resid = jnp.where(inside, signal - smooth, 0.0)
    mixed = lax.all_to_all(resid, "series", split_axis=1, concat_axis=0, tiled=True)
    full = lax.psum(cross_rows(mixed, mixed), ("tm", "series"))
    gram = lax.dynamic_slice_in_dim(full, group, rows)
    correlation = (
        jnp.minimum(last, valid_end[None, :]) - jnp.maximum(first, valid_start[None, :])
    ).astype(jnp.float32)
    return (smooth, slope, gram / correlation)


def solution(mesh):
    in_specs = (P("series", "tm"), P(), P())
    out_specs = (P("series", "tm"), P("series", "tm"), P("series", None))
    return jax.shard_map(shards, mesh=mesh, in_specs=in_specs, out_specs=out_specs, check_vma=False)
```

profile of v0, /device:TPU:0, one launch (start us, length us, event | category | flops | bytes accessed | tf_op | source)
XLA Modules:
  0.0 258.8 jit_solution(5672851760717426179)
XLA Ops:
  0.6 0.8 fusion.14
  1.4 4.9 %collective-permute-start = (f32[16,32]{1,0:T(8,128)S(1)}, f32[16,32]{1,0:T(8,128)S(1)}, u32[]{:S(2)}, u32[]{:S(2)}) collective-permute-start(f32[16,32]{1,0:T(8,128)S(1)} %get-tuple-element.11), channel_id=1, source_target_pairs={{0,4},{4,8},{8,12},{12,16},{16,20},{20,24},{24,28},{1,5},{5,9},{9,... | collective-permute-start | bytes 6152 | tf_op jit(solution)/shard_map/ppermute | solution.py:17
  6.3 1.3 collective-permute-start.1
  7.6 0.6 multiply_reduce_fusion.1
  8.9 0.7 multiply_reduce_fusion
  9.6 0.7 fusion.18
  10.3 0.7 fusion.17
  11.0 0.7 fusion.16
  11.7 0.7 fusion.15
  12.4 0.0 copy-start.1
  12.4 0.0 copy-start
  12.4 3.1 %constant_dynamic-update-slice_fusion.1 = f32[16,32800]{1,0:T(8,128)} fusion(f32[16,32768]{1,0:T(8,128)} %param.5), kind=kLoop, calls=%fused_computation.27 | loop fusion | bytes 4194304
  15.5 0.0 copy-done.1
  15.5 0.1 broadcast_add_fusion.1
  15.6 0.0 copy-done
  15.6 0.1 broadcast_add_fusion
  103.3 0.0 collective-permute-done
  103.3 0.3 dynamic-update-slice.2
  103.6 6.4 %dynamic-update-slice.3 = f32[16,32832]{1,0:T(8,128)S(1)} dynamic-update-slice(f32[16,32832]{1,0:T(8,128)S(1)} %dynamic-update-slice.2, f32[16,32768]{1,0:T(8,128)} %param.5, s32[]{} %constant.163, s32[]{} %constant.165) | dynamic-update-slice | bytes 4194308
  109.9 0.0 collective-permute-done.1
  109.9 0.6 constant_dynamic-update-slice_fusion
  110.5 0.2 dynamic-update-slice.4
  110.7 19.9 %multiply_add_fusion.1 = f32[16,32800]{1,0:T(8,128)} fusion(f32[16,32800]{1,0:T(8,128)} %constant_dynamic-update-slice_fusion, f32[16,32832]{1,0:T(8,128)S(1)} %dynamic-update-slice.4, f32[16,32768]{1,0:T(8,128)} %param.5, f32[16,32]{1,0:T(8,128)S(1)} %collective-permute-done, f32[]{:T(128)S(6)} %div.236, f32[]{:T(128)S(6)} %div.235, f32[]{:T(128)S(6)} %div.234, ...), kind=kLoop, calls=%fused_computation.15 | loop fusion | flops 34636800 | bytes 71372928 | tf_op jit(solution)/shard_map/add | solution.py:56
  130.6 1.6 gather_fusion.3
  132.2 1.5 gather_fusion.2
  133.7 20.0 %add_multiply_fusion = f32[16,32800]{1,0:T(8,128)} fusion(f32[16,32800]{1,0:T(8,128)} %constant_dynamic-update-slice_fusion, f32[16,32832]{1,0:T(8,128)S(1)} %dynamic-update-slice.4, f32[16,32768]{1,0:T(8,128)} %param.5, f32[16,32]{1,0:T(8,128)S(1)} %collective-permute-done), kind=kLoop, calls=%fused_computation.13 | loop fusion | flops 17843200 | bytes 71372800 | tf_op jit(solution)/shard_map/add | solution.py:55
  153.8 1.6 gather_fusion.1
  155.4 1.5 gather_fusion
  156.9 19.9 %multiply_add_fusion = f32[16,32800]{1,0:T(8,128)} fusion(f32[16,32800]{1,0:T(8,128)} %constant_dynamic-update-slice_fusion, f32[16,32832]{1,0:T(8,128)S(1)} %dynamic-update-slice.4, f32[16,32768]{1,0:T(8,128)} %param.5, f32[16,32]{1,0:T(8,128)S(1)} %collective-permute-done, f32[]{:T(128)S(6)} %div.270, f32[]{:T(128)S(6)} %div.269, f32[]{:T(128)S(6)} %div.268, ...), kind=kLoop, calls=%fused_computation.14 | loop fusion | flops 34636800 | bytes 71372928 | tf_op jit(solution)/shard_map/add | solution.py:57
  176.8 1.6 gather_fusion.5
  178.4 1.5 gather_fusion.4
  180.0 6.0 %subtract_select_fusion = (f32[16,32768]{1,0:T(8,128)S(1)}, f32[16,32768]{1,0:T(8,128)}, f32[16,32768]{1,0:T(8,128)}) fusion(f32[16,32768]{1,0:T(8,128)} %param.5, s32[32768]{0:T(1024)S(1)} %iota_add_fusion, s32[16]{0:T(128)S(1)} %get-tuple-element.9, s32[16]{0:T(128)S(1)} %get-tuple-element.7, f32[]{:T(128)S(6)} %div.237, f32[16,32800]{1,0:T(8,128)} %multiply_add_fusion, ...), kind=kLoop, calls=%fused_computation.20 | loop fusion | flops 15204352 | bytes 14811780 | tf_op jit(solution)/shard_map/jit(_where)/select_n | solution.py:89
  185.9 0.1 copy.9
  186.1 28.4 %all_to_all.19 = f32[16,4,8192]{2,0,1:T(8,128)S(1)} all-to-all(f32[16,4,8192]{2,0,1:T(8,128)S(1)} %bitcast.161), channel_id=1, replica_groups=mesh['tm'=8,'series'=4] {'series'}, dimensions={1} | all-to-all | bytes 4194304 | tf_op jit(solution)/shard_map/all_to_all | solution.py:90
  214.5 1.8 fusion.19
  216.3 41.8 %psum.7 = f32[64,64]{1,0:T(8,128)S(1)} all-reduce(f32[64,64]{1,0:T(8,128)S(1)} %fusion.19), channel_id=1, replica_groups=mesh['tm'=8,'series'=4] {'tm','series'}, use_global_device_ids=true, to_apply=%region_2.4 | all-reduce | flops 4096 | bytes 32768 | tf_op jit(solution)/shard_map/psum | solution.py:91
  258.1 0.7 convert_divide_fusion
  (11 shorter events, 0.1 us)
Async XLA Ops:
  1.4 101.8 %collective-permute-start = (f32[16,32]{1,0:T(8,128)S(1)}, f32[16,32]{1,0:T(8,128)S(1)}, u32[]{:S(2)}, u32[]{:S(2)}) collective-permute-start(f32[16,32]{1,0:T(8,128)S(1)} %get-tuple-element.11), channel_id=1, source_target_pairs={{0,4},{4,8},{8,12},{12,16},{16,20},{20,24},{24,28},{1,5},{5,9},{9,... | collective-permute-start | bytes 6152 | tf_op jit(solution)/shard_map/ppermute | solution.py:17
  6.3 103.6 %collective-permute-start.1 = (f32[16,32]{1,0:T(8,128)S(1)}, f32[16,32]{1,0:T(8,128)S(1)}, u32[]{:S(2)}, u32[]{:S(2)}) collective-permute-start(f32[16,32]{1,0:T(8,128)S(1)} %get-tuple-element.12), channel_id=1, source_target_pairs={{4,0},{8,4},{12,8},{16,12},{20,16},{24,20},{28,24},{5,1},{9,5},{13... | collective-permute-start | bytes 6152 | tf_op jit(solution)/shard_map/ppermute | solution.py:19
  12.4 3.1 %copy-start.1 = (s32[64]{0:T(128)S(1)}, s32[64]{0:T(128)}, u32[]{:S(2)}) copy-start(s32[64]{0:T(128)} %param.6) | copy-start | bytes 772
  12.4 3.2 %copy-start = (s32[64]{0:T(128)S(1)}, s32[64]{0:T(128)}, u32[]{:S(2)}) copy-start(s32[64]{0:T(128)} %param.7) | copy-start | bytes 772
where the time goes:
time: 261 us; the launch traced here: 259 us
  between operations  88.9 us (34%)
  blocking collectives  70.3 us (27%)
  other arithmetic  68 us (26%)
  local copies, waits for them, and re-layouts  23.7 us (9%)
  starting transfers between devices  6.18 us (2%)
    psum x1, blocking collectives, shards(): full = lax.psum(cross_rows(mixed, mixed), ('tm', 'series'))  41.8 us
    all_to_all x1, blocking collectives, shards(): lax.all_to_all(resid, 'series', split_axis=1, concat_axis=0, tiled=True)  28.4 us
    add x1, other arithmetic, shards(): level = level + window * (1.0 / taps)  20 us
    add x1, other arithmetic, shards(): tilt = tilt + window * (offsets[m] / second)  19.9 us
    add x1, other arithmetic, shards(): bend = bend + window * (curved[m] / fourth)  19.9 us
    unnamed x7, local copies, waits for them, and re-layouts  9.73 us
    gather x6, local copies, waits for them, and re-layouts, held_value(): return jnp.take_along_axis(field, spot, axis=1)  9.43 us
    select_n x1, other arithmetic, shards(): resid = jnp.where(inside, signal - smooth, 0.0)  5.98 us
  transfers between devices with their start and end apart: 2, of which 0 were waited for; matrix products, arithmetic and copies ran while one was open for 5% of the time, Pallas kernels for 0%

commit v1 on v0

v1 whole, which is shorter than its diff:
```python
import functools

import jax
import jax.numpy as jnp
from jax import lax
from jax.experimental import pallas as pl
from jax.experimental.pallas import tpu as pltpu
from jax.sharding import PartitionSpec as P

HALF = 16
LANE = 128
TAPS = 2 * HALF + 1
SECOND = float(sum(j * j for j in range(-HALF, HALF + 1)))
CENTRE_SQ = SECOND / TAPS
FOURTH = float(sum((j * j - CENTRE_SQ) ** 2 for j in range(-HALF, HALF + 1)))
MESH = pl.DeviceIdType.MESH


def chunk_of(quarter):
    chunk = 2048
    while quarter % chunk:
        chunk //= 2
    return chunk


def kernel(
    n_s, n_t, rows, width, chunk,
    vs_hbm, ve_hbm, sig_hbm,
    smooth, slope, cov,
    vs, ve, ext, wts, wins, coef, ends, res, mixed, halo, part, r1, mine, r2,
    load_sem, bound_sem, halo_send, halo_recv, send_sem, recv_sem, s1_send, s1_recv, s2_send, s2_recv,
):
    s = lax.axis_index("series")
    t = lax.axis_index("tm")
    quarter = width // n_s
    per = quarter // chunk
    steps = n_s * per
    sends = (n_s - 1) * per
    total = n_s * rows
    f32 = jnp.float32

    load = pltpu.make_async_copy(sig_hbm, ext.at[:, pl.ds(LANE, width)], load_sem)
    load.start()
    starts = pltpu.make_async_copy(vs_hbm, vs, bound_sem.at[0])
    stops = pltpu.make_async_copy(ve_hbm, ve, bound_sem.at[1])
    starts.start()
    stops.start()
    barrier = pltpu.get_barrier_semaphore()
    for d in range(1, n_s):
        pl.semaphore_signal(barrier, inc=1, device_id={"series": lax.rem(s + d, n_s)}, device_id_type=MESH)
    for d in range(1, n_t):
        pl.semaphore_signal(barrier, inc=1, device_id={"tm": lax.rem(t + d, n_t)}, device_id_type=MESH)

    tap = lax.broadcasted_iota(jnp.int32, (2 * LANE, LANE), 0) - lax.broadcasted_iota(jnp.int32, (2 * LANE, LANE), 1) - HALF
    near = (tap >= -HALF) & (tap <= HALF)
    tap = tap.astype(f32)
    wts[:, :LANE] = jnp.where(near, 1.0 / TAPS - (tap * tap - CENTRE_SQ) * (CENTRE_SQ / FOURTH), 0.0)
    wts[:, LANE:] = jnp.where(near, tap * (HALF / SECOND), 0.0)
    ext[:, :LANE] = jnp.zeros((rows, LANE), f32)
    ext[:, LANE + width :] = jnp.zeros((rows, LANE), f32)

    starts.wait()
    stops.wait()
    row = lax.broadcasted_iota(jnp.int32, (rows, LANE), 0)
    begin = t * width
    first = jnp.zeros((rows, LANE), jnp.int32)
    last = jnp.zeros((rows, LANE), jnp.int32)
    for i in range(rows):
        first = jnp.where(row == i, vs[s * rows + i], first)
        last = jnp.where(row == i, ve[s * rows + i], last)
    ends[0] = first - begin
    ends[1] = last - begin

    def spots():
        low = ends[0] + LANE
        high = ends[1] - TAPS + LANE
        return low, high

    def tile_of(spot):
        return lax.shift_right_arithmetic(spot, LANE.bit_length() - 1)

    def collect(n, tile, wins):
        low, high = spots()
        wins = list(wins)
        for side, spot in ((0, low), (1, high)):
            wins[2 * side] = jnp.where(tile_of(spot) == n, tile, wins[2 * side])
            wins[2 * side + 1] = jnp.where(tile_of(spot) == n - 1, tile, wins[2 * side + 1])
        return tuple(wins)

    def held(wins):
        lanes = lax.broadcasted_iota(jnp.int32, (rows, LANE), 1)
        for side, spot in enumerate(spots()):
            off = spot - tile_of(spot) * LANE + HALF
            near, far = lanes - off, lanes + LANE - off
            sums = []
            for j, win in ((near, wins[2 * side]), (far, wins[2 * side + 1])):
                win = jnp.where((j >= -HALF) & (j <= HALF), win, 0.0)
                j = j.astype(f32)
                sums.append((win, win * j, win * (j * j - CENTRE_SQ)))
            for m, scale in enumerate((1.0 / TAPS, 1.0 / SECOND, 1.0 / FOURTH)):
                value = jnp.sum(sums[0][m] + sums[1][m], axis=1, keepdims=True) * scale
                coef[3 * side + m] = jnp.broadcast_to(value, (rows, LANE))

    load.wait()

    group = 8
    while (width // LANE) % group:
        group //= 2

    def gather(g, found):
        for n in range(group):
            at = g * group + n
            found = collect(at + 1, ext[:, pl.ds(pl.multiple_of((at + 1) * LANE, LANE), LANE)], found)
        return found

    found = lax.fori_loop(0, width // LANE // group, gather, (jnp.zeros((rows, LANE), f32),) * 4)
    for w in range(4):
        wins[w] = found[w]
    held(found)
    pl.semaphore_wait(barrier, n_s - 1 + n_t - 1)

    right, left = lax.rem(t + 1, n_t), lax.rem(t + n_t - 1, n_t)
    to_right = pltpu.make_async_remote_copy(
        ext.at[:, pl.ds(width, LANE)], halo.at[0], halo_send.at[0], halo_recv.at[0],
        device_id={"tm": right}, device_id_type=MESH)
    to_left = pltpu.make_async_remote_copy(
        ext.at[:, pl.ds(LANE, LANE)], halo.at[1], halo_send.at[1], halo_recv.at[1],
        device_id={"tm": left}, device_id_type=MESH)
    to_right.start()
    to_left.start()

    def offset(qi):
        if n_s == 4:
            odd = lax.rem(s, 2)
            return jnp.where(qi == 0, 2, jnp.where(qi == 1, 3 - 2 * odd, jnp.where(qi == 2, 1 + 2 * odd, 0)))
        return lax.rem(qi + 1, n_s)

    def place(k):
        qi = k // per
        q = lax.rem(s + offset(qi), n_s)
        j = lax.rem(lax.rem(k, per) + jnp.where(q == 0, 1, 0), per)
        return q, j

    def transfer(k):
        q, j = place(k)
        return pltpu.make_async_remote_copy(
            res.at[:, pl.ds(pl.multiple_of(q * quarter + j * chunk, chunk), chunk)],
            mixed.at[s, :, pl.ds(pl.multiple_of(j * chunk, chunk), chunk)],
            send_sem.at[k], recv_sem.at[k],
            device_id={"series": q}, device_id_type=MESH)

    tiles = chunk // LANE

    def spread(v):
        return jnp.concatenate([v] * tiles, axis=1)

    def step(k, carry):
        @pl.when(k == per - 1)
        def _():
            to_right.wait_recv()
            to_left.wait_recv()
            before = jnp.where(t == 0, 0.0, halo[0])
            after = jnp.where(t == n_t - 1, 0.0, halo[1])
            ext[:, :LANE] = before
            ext[:, LANE + width :] = after
            final = tuple(wins[w] for w in range(4))
            final = collect(0, before, final)
            held(collect(width // LANE + 1, after, final))

        q, j = place(k)
        base = pl.multiple_of(q * quarter + j * chunk, chunk)
        v = ext[:, pl.ds(base, chunk + 2 * LANE)]
        moved = pltpu.roll(v, chunk + LANE + HALF, 1)
        lines = jnp.concatenate([moved[:, n * LANE : (n + 2) * LANE] for n in range(tiles)], axis=0)
        out = jnp.dot(lines, wts[...], precision=lax.Precision.HIGHEST, preferred_element_type=f32)
        sm = jnp.concatenate([out[n * rows : (n + 1) * rows, :LANE] for n in range(tiles)], axis=1)
        sl = jnp.concatenate([out[n * rows : (n + 1) * rows, LANE:] for n in range(tiles)], axis=1)
        moment = base + lax.broadcasted_iota(jnp.int32, (rows, chunk), 1)
        low = moment - spread(ends[0])
        high = moment - spread(ends[1])
        inside = (low >= 0) & (high < 0)
        below = low < HALF
        above = high >= -HALF
        along = jnp.where(below, low - HALF, high + HALF + 1).astype(f32)
        lv = jnp.where(below, spread(coef[0]), spread(coef[3]))
        tl = jnp.where(below, spread(coef[1]), spread(coef[4]))
        bd = jnp.where(below, spread(coef[2]), spread(coef[5]))
        end = below | above
        sm = jnp.where(end, lv + tl * along + bd * (along * along - CENTRE_SQ), sm)
        sl = jnp.where(end, HALF * (tl + 2.0 * along * bd), sl)
        sm = jnp.where(inside, sm, 0.0)
        smooth[:, pl.ds(base, chunk)] = sm
        slope[:, pl.ds(base, chunk)] = jnp.where(inside, sl, 0.0)
        rs = jnp.where(inside, v[:, LANE : LANE + chunk] - sm, 0.0)

        @pl.when(k < sends)
        def _():
            res[:, pl.ds(base, chunk)] = rs

        @pl.when(k >= sends)
        def _():
            mixed[s, :, pl.ds(pl.multiple_of(j * chunk, chunk), chunk)] = rs

        @pl.when((k >= 1) & (k <= sends))
        def _():
            transfer(k - 1).start()

        return carry

    lax.fori_loop(0, steps, step, 0)

    def arrival(k, i):
        src = lax.rem(s + n_s - offset(k // per), n_s)
        j = lax.rem(i + jnp.where(s == 0, 1, 0), per)
        return pltpu.make_async_remote_copy(
            res.at[:, pl.ds(0, chunk)],
            mixed.at[src, :, pl.ds(pl.multiple_of(j * chunk, chunk), chunk)],
            send_sem.at[k], recv_sem.at[k],
            device_id={"series": src}, device_id_type=MESH)

    gram = jnp.zeros((2 * total, 2 * total), f32)
    for i in range(per):
        for qi in range(n_s - 1):
            arrival(qi * per + i, i).wait_recv()
        j = lax.rem(i + jnp.where(s == 0, 1, 0), per)
        x = jnp.concatenate(
            [mixed[g, :, pl.ds(pl.multiple_of(j * chunk, chunk), chunk)] for g in range(n_s)], axis=0)
        hi = x.astype(jnp.bfloat16)
        lo = (x - hi.astype(f32)).astype(jnp.bfloat16)
        z = jnp.concatenate([hi, lo], axis=0)
        gram = gram + lax.dot_general(z, z, (((1,), (1,)), ((), ())), preferred_element_type=f32)
    both = gram[:total] + gram[total:]
    both = both + pltpu.roll(both, total, 1)
    for g in range(n_s):
        part[g] = both[g * rows : (g + 1) * rows]

    def first_stage(d):
        peer = lax.rem(s + d, n_s)
        return pltpu.make_async_remote_copy(
            part.at[peer], r1.at[d - 1], s1_send.at[d - 1], s1_recv.at[d - 1],
            device_id={"series": peer}, device_id_type=MESH)

    for d in range(1, n_s):
        first_stage(d).start()

    lane = lax.broadcasted_iota(jnp.int32, (rows, 2 * total), 1)
    first_k = jnp.zeros((rows, 2 * total), jnp.int32)
    last_k = jnp.zeros((rows, 2 * total), jnp.int32)
    for i in range(total):
        first_k = jnp.where(lane == i, vs[i], first_k)
        last_k = jnp.where(lane == i, ve[i], last_k)
    count = (jnp.minimum(last_k, last) - jnp.maximum(first_k, first)).astype(f32)

    own = part[s]
    for d in range(1, n_s):
        first_stage(d).wait_recv()
        own = own + r1[d - 1]
    mine[...] = own

    def second_stage(d):
        return pltpu.make_async_remote_copy(
            mine, r2.at[t], s2_send.at[d - 1], s2_recv.at[d - 1],
            device_id={"tm": lax.rem(t + d, n_t)}, device_id_type=MESH)

    def second_arrival(d):
        src = lax.rem(t + n_t - d, n_t)
        return pltpu.make_async_remote_copy(
            mine, r2.at[src], s2_send.at[d - 1], s2_recv.at[d - 1],
            device_id={"tm": src}, device_id_type=MESH)

    for d in range(1, n_t):
        second_stage(d).start()
    r2[t] = own
    for k in range(sends):
        transfer(k).wait_send()
    to_right.wait_send()
    to_left.wait_send()
    for d in range(1, n_s):
        first_stage(d).wait_send()
    for d in range(1, n_t):
        second_arrival(d).wait_recv()
    full = r2[0]
    for d in range(1, n_t):
        full = full + r2[d]
    cov[...] = (full / count)[:, :total]
    for d in range(1, n_t):
        second_stage(d).wait_send()


def solution(mesh):
    n_t, n_s = mesh.shape["tm"], mesh.shape["series"]

    def shards(signal, valid_start, valid_end):
        rows, width = signal.shape
        total = rows * n_s
        quarter = width // n_s
        chunk = chunk_of(quarter)
        sends = (n_s - 1) * (quarter // chunk)
        f32 = jnp.float32
        dma = pltpu.SemaphoreType.DMA
        return pl.pallas_call(
            functools.partial(kernel, n_s, n_t, rows, width, chunk),
            out_shape=(
                jax.ShapeDtypeStruct((rows, width), f32),
                jax.ShapeDtypeStruct((rows, width), f32),
                jax.ShapeDtypeStruct((rows, total), f32),
            ),
            in_specs=[
                pl.BlockSpec(memory_space=pltpu.HBM),
                pl.BlockSpec(memory_space=pltpu.HBM),
                pl.BlockSpec(memory_space=pltpu.HBM),
            ],
            out_specs=(pl.BlockSpec(memory_space=pltpu.VMEM),) * 3,
            scratch_shapes=[
                pltpu.SMEM((total,), jnp.int32),
                pltpu.SMEM((total,), jnp.int32),
                pltpu.VMEM((rows, width + 2 * LANE), f32),
                pltpu.VMEM((2 * LANE, 2 * LANE), f32),
                pltpu.VMEM((4, rows, LANE), f32),
                pltpu.VMEM((6, rows, LANE), f32),
                pltpu.VMEM((2, rows, LANE), jnp.int32),
                pltpu.VMEM((rows, width), f32),
                pltpu.VMEM((n_s, rows, quarter), f32),
                pltpu.VMEM((2, rows, LANE), f32),
                pltpu.VMEM((n_s, rows, 2 * total), f32),
                pltpu.VMEM((n_s - 1, rows, 2 * total), f32),
                pltpu.VMEM((rows, 2 * total), f32),
                pltpu.VMEM((n_t, rows, 2 * total), f32),
                dma,
                dma((2,)),
                dma((2,)),
                dma((2,)),
                dma((sends,)),
                dma((sends,)),
                dma((n_s - 1,)),
                dma((n_s - 1,)),
                dma((n_t - 1,)),
                dma((n_t - 1,)),
            ],
            compiler_params=pltpu.CompilerParams(
                collective_id=0, has_side_effects=True, vmem_limit_bytes=67043328 - 8 * rows * width - rows * width
            ),
        )(valid_start, valid_end, signal)

    in_specs = (P("series", "tm"), P(), P())
    out_specs = (P("series", "tm"), P("series", "tm"), P("series", None))
    return jax.shard_map(shards, mesh=mesh, in_specs=in_specs, out_specs=out_specs, check_vma=False)
```

time: 261 us -> 45.9 us (0.18)
  between operations: 88.9 us -> 0.65 us
  blocking collectives: 70.3 us -> 0 us
  other arithmetic: 68 us -> 0 us
  Pallas kernels: 0 us -> 39.9 us
  local copies, waits for them, and re-layouts: 23.7 us -> 5.12 us
  starting transfers between devices: 6.18 us -> 0 us
    add x5 -> x0, other arithmetic: 59.9 us -> none  [the longest x1 20 us: shards(): level = level + window * (1.0 / taps)]
    psum x1 -> x0, blocking collectives: 41.8 us -> none  [shards(): full = lax.psum(cross_rows(mixed, mixed), ('tm', 'series'))]
    pallas_call x0 -> x1, Pallas kernels: none -> 39.9 us  [shards(): pl.pallas_call(functools.partial(kernel, n_s, n_t, rows, width, chunk), o...]
    all_to_all x1 -> x0, blocking collectives: 28.4 us -> none  [shards(): lax.all_to_all(resid, 'series', split_axis=1, concat_axis=0, tiled=True)]
    gather x6 -> x0, local copies, waits for them, and re-layouts: 9.43 us -> none  [held_value(): return jnp.take_along_axis(field, spot, axis=1)]
    ppermute x2 -> x0, starting transfers between devices: 6.18 us -> none  [the longest x1 4.89 us: padded(): lax.ppermute(tail, axis, [(i, (i + 1) % count) for i in range(ends)])]
    select_n x1 -> x0, other arithmetic: 5.98 us -> none  [shards(): resid = jnp.where(inside, signal - smooth, 0.0)]
    unnamed x7, local copies, waits for them, and re-layouts: 9.73 us -> 5.12 us
  transfers between devices with their start and end apart: 2 -> 0, of which waited for: 0 -> 0; matrix products, arithmetic and copies ran while one was open for 5% -> 0% of each run, Pallas kernels for 0% -> 0%
where the time goes in v1:
time: 45.9 us; the launch traced here: 45.7 us
  Pallas kernels  39.9 us (87%)
  local copies, waits for them, and re-layouts  5.12 us (11%)
  between operations  0.65 us (1%)
    pallas_call x1, Pallas kernels, shards(): pl.pallas_call(functools.partial(kernel, n_s, n_t, rows, width, chunk), o...  39.9 us
    unnamed x7, local copies, waits for them, and re-layouts  5.12 us

profile of v1, /device:TPU:0, one launch (start us, length us, event | category | flops | bytes accessed | tf_op | source)
XLA Modules:
  0.0 45.7 jit_solution(11055546571876373613)
XLA Ops:
  0.6 39.9 %shard_map.58 = (f32[16,32768]{1,0:T(8,128)}, f32[16,32768]{1,0:T(8,128)}, f32[16,64]{1,0:T(8,128)}) custom-call(s32[64]{0:T(128)} %vs_hbm.1, s32[64]{0:T(128)} %ve_hbm.1, f32[16,32768]{1,0:T(8,128)} %sig_hbm.1), custom_call_target="tpu_custom_call" | custom-call | tf_op jit(solution)/shard_map/pallas_call | solution.py:301
  40.6 0.0 copy-start
  40.6 3.2 %copy.9 = f32[16,32768]{1,0:T(8,128)} copy(f32[16,32768]{1,0:T(8,128)} %get-tuple-element.6) | data formatting | bytes 4194304
  43.8 0.0 copy-done
  43.8 0.0 copy-start.1
  43.8 1.3 %copy.10 = f32[16,32768]{1,0:T(8,128)} copy(f32[16,32768]{1,0:T(8,128)S(1)} %copy-done) | data formatting | bytes 4194304
  45.1 0.0 copy-done.1
  45.1 0.6 %copy.11 = f32[16,64]{1,0:T(8,128)} copy(f32[16,64]{1,0:T(8,128)S(1)} %copy-done.1) | data formatting | bytes 8192
Async XLA Ops:
  40.6 3.2 %copy-start = (f32[16,32768]{1,0:T(8,128)S(1)}, f32[16,32768]{1,0:T(8,128)}, u32[]{:S(2)}) copy-start(f32[16,32768]{1,0:T(8,128)} %get-tuple-element.7) | copy-start | bytes 6291460
  43.8 1.3 %copy-start.1 = (f32[16,64]{1,0:T(8,128)S(1)}, f32[16,64]{1,0:T(8,128)}, u32[]{:S(2)}) copy-start(f32[16,64]{1,0:T(8,128)} %get-tuple-element.8) | copy-start | bytes 12292

commit v2 on v1

--- a/solution.py
+++ b/solution.py
@@ -17,7 +17,7 @@
 
 
 def chunk_of(quarter):
-    chunk = 2048
+    chunk = 1024
     while quarter % chunk:
         chunk //= 2
     return chunk
@@ -27,7 +27,7 @@
     n_s, n_t, rows, width, chunk,
     vs_hbm, ve_hbm, sig_hbm,
     smooth, slope, cov,
-    vs, ve, ext, wts, wins, coef, ends, res, mixed, halo, part, r1, mine, r2,
+    vs, ve, ext, wts, ends, res, mixed, halo, part, r1, mine, r2,
     load_sem, bound_sem, halo_send, halo_recv, send_sem, recv_sem, s1_send, s1_recv, s2_send, s2_recv,
 ):
     s = lax.axis_index("series")
@@ -37,14 +37,28 @@
     steps = n_s * per
     sends = (n_s - 1) * per
     total = n_s * rows
+    tiles = chunk // LANE
     f32 = jnp.float32
 
-    load = pltpu.make_async_copy(sig_hbm, ext.at[:, pl.ds(LANE, width)], load_sem)
-    load.start()
     starts = pltpu.make_async_copy(vs_hbm, vs, bound_sem.at[0])
     stops = pltpu.make_async_copy(ve_hbm, ve, bound_sem.at[1])
     starts.start()
     stops.start()
+    def offset(qi):
+        if n_s == 4:
+            odd = lax.rem(s, 2)
+            return jnp.where(qi == 0, 2, jnp.where(qi == 1, 3 - 2 * odd, jnp.where(qi == 2, 1 + 2 * odd, 0)))
+        return lax.rem(qi + 1, n_s)
+
+    def load(qi):
+        q = lax.rem(s + offset(qi), n_s)
+        return pltpu.make_async_copy(
+            sig_hbm.at[:, pl.ds(pl.multiple_of(q * quarter, LANE), quarter)],
+            ext.at[:, pl.ds(pl.multiple_of(q * quarter + LANE, LANE), quarter)],
+            load_sem.at[qi])
+
+    for qi in range(n_s):
+        load(qi).start()
     barrier = pltpu.get_barrier_semaphore()
     for d in range(1, n_s):
         pl.semaphore_signal(barrier, inc=1, device_id={"series": lax.rem(s + d, n_s)}, device_id_type=MESH)
@@ -71,53 +85,26 @@
     ends[0] = first - begin
     ends[1] = last - begin
 
-    def spots():
-        low = ends[0] + LANE
-        high = ends[1] - TAPS + LANE
-        return low, high
-
-    def tile_of(spot):
-        return lax.shift_right_arithmetic(spot, LANE.bit_length() - 1)
-
-    def collect(n, tile, wins):
-        low, high = spots()
-        wins = list(wins)
-        for side, spot in ((0, low), (1, high)):
-            wins[2 * side] = jnp.where(tile_of(spot) == n, tile, wins[2 * side])
-            wins[2 * side + 1] = jnp.where(tile_of(spot) == n - 1, tile, wins[2 * side + 1])
-        return tuple(wins)
-
-    def held(wins):
+    def held(v, base):
         lanes = lax.broadcasted_iota(jnp.int32, (rows, LANE), 1)
-        for side, spot in enumerate(spots()):
-            off = spot - tile_of(spot) * LANE + HALF
-            near, far = lanes - off, lanes + LANE - off
+        found = []
+        for spot in (ends[0] + LANE - base, ends[1] - TAPS + LANE - base):
+            tile = lax.shift_right_arithmetic(spot, LANE.bit_length() - 1)
+            pair = [jnp.zeros((rows, LANE), f32)] * 2
+            for n in range(tiles + 1):
+                here = tile == n
+                for w in range(2):
+                    pair[w] = jnp.where(here, v[:, (n + w) * LANE : (n + w + 1) * LANE], pair[w])
+            j = lanes - (spot - tile * LANE + HALF)
             sums = []
-            for j, win in ((near, wins[2 * side]), (far, wins[2 * side + 1])):
+            for j, win in ((j, pair[0]), (j + LANE, pair[1])):
                 win = jnp.where((j >= -HALF) & (j <= HALF), win, 0.0)
                 j = j.astype(f32)
                 sums.append((win, win * j, win * (j * j - CENTRE_SQ)))
             for m, scale in enumerate((1.0 / TAPS, 1.0 / SECOND, 1.0 / FOURTH)):
                 value = jnp.sum(sums[0][m] + sums[1][m], axis=1, keepdims=True) * scale
-                coef[3 * side + m] = jnp.broadcast_to(value, (rows, LANE))
-
-    load.wait()
-
-    group = 8
-    while (width // LANE) % group:
-        group //= 2
-
-    def gather(g, found):
-        for n in range(group):
-            at = g * group + n
-            found = collect(at + 1, ext[:, pl.ds(pl.multiple_of((at + 1) * LANE, LANE), LANE)], found)
+                found.append(jnp.broadcast_to(value, (rows, LANE)))
         return found
-
-    found = lax.fori_loop(0, width // LANE // group, gather, (jnp.zeros((rows, LANE), f32),) * 4)
-    for w in range(4):
-        wins[w] = found[w]
-    held(found)
-    pl.semaphore_wait(barrier, n_s - 1 + n_t - 1)
 
     right, left = lax.rem(t + 1, n_t), lax.rem(t + n_t - 1, n_t)
     to_right = pltpu.make_async_remote_copy(
@@ -126,19 +113,10 @@
     to_left = pltpu.make_async_remote_copy(
         ext.at[:, pl.ds(LANE, LANE)], halo.at[1], halo_send.at[1], halo_recv.at[1],
         device_id={"tm": left}, device_id_type=MESH)
-    to_right.start()
-    to_left.start()
-
-    def offset(qi):
-        if n_s == 4:
-            odd = lax.rem(s, 2)
-            return jnp.where(qi == 0, 2, jnp.where(qi == 1, 3 - 2 * odd, jnp.where(qi == 2, 1 + 2 * odd, 0)))
-        return lax.rem(qi + 1, n_s)
-
     def place(k):
         qi = k // per
         q = lax.rem(s + offset(qi), n_s)
-        j = lax.rem(lax.rem(k, per) + jnp.where(q == 0, 1, 0), per)
+        j = lax.rem(lax.rem(k, per) + 1, per)
         return q, j
 
     def transfer(k):
@@ -149,23 +127,25 @@
             send_sem.at[k], recv_sem.at[k],
             device_id={"series": q}, device_id_type=MESH)
 
-    tiles = chunk // LANE
-
     def spread(v):
         return jnp.concatenate([v] * tiles, axis=1)
 
     def step(k, carry):
-        @pl.when(k == per - 1)
+        @pl.when(k == 0)
+        def _():
+            load(0).wait()
+
+        @pl.when(k == 1)
+        def _():
+            for qi in range(1, n_s):
+                load(qi).wait()
+
+        @pl.when(k == per - 2)
         def _():
             to_right.wait_recv()
             to_left.wait_recv()
-            before = jnp.where(t == 0, 0.0, halo[0])
-            after = jnp.where(t == n_t - 1, 0.0, halo[1])
-            ext[:, :LANE] = before
-            ext[:, LANE + width :] = after
-            final = tuple(wins[w] for w in range(4))
-            final = collect(0, before, final)
-            held(collect(width // LANE + 1, after, final))
+            ext[:, :LANE] = jnp.where(t == 0, 0.0, halo[0])
+            ext[:, LANE + width :] = jnp.where(t == n_t - 1, 0.0, halo[1])
 
         q, j = place(k)
         base = pl.multiple_of(q * quarter + j * chunk, chunk)
@@ -178,6 +158,7 @@
         moment = base + lax.broadcasted_iota(jnp.int32, (rows, chunk), 1)
         low = moment - spread(ends[0])
         high = moment - spread(ends[1])
+        coef = held(v, base)
         inside = (low >= 0) & (high < 0)
         below = low < HALF
         above = high >= -HALF
@@ -201,6 +182,15 @@
         def _():
             mixed[s, :, pl.ds(pl.multiple_of(j * chunk, chunk), chunk)] = rs
 
+        @pl.when(k == 0)
+        def _():
+            pl.semaphore_wait(barrier, n_s - 1 + n_t - 1)
+
+        @pl.when(k == 1)
+        def _():
+            to_right.start()
+            to_left.start()
+
         @pl.when((k >= 1) & (k <= sends))
         def _():
             transfer(k - 1).start()
@@ -211,18 +201,24 @@
 
     def arrival(k, i):
         src = lax.rem(s + n_s - offset(k // per), n_s)
-        j = lax.rem(i + jnp.where(s == 0, 1, 0), per)
+        j = (i + 1) % per
         return pltpu.make_async_remote_copy(
             res.at[:, pl.ds(0, chunk)],
             mixed.at[src, :, pl.ds(pl.multiple_of(j * chunk, chunk), chunk)],
             send_sem.at[k], recv_sem.at[k],
             device_id={"series": src}, device_id_type=MESH)
 
+    half = rows // 2
+    left_half = lax.broadcasted_iota(jnp.int32, (half, 2 * total), 1) < total
+
+    def pack(v):
+        return jnp.where(left_half, v[:half], v[half:])
+
     gram = jnp.zeros((2 * total, 2 * total), f32)
     for i in range(per):
         for qi in range(n_s - 1):
             arrival(qi * per + i, i).wait_recv()
-        j = lax.rem(i + jnp.where(s == 0, 1, 0), per)
+        j = (i + 1) % per
         x = jnp.concatenate(
             [mixed[g, :, pl.ds(pl.multiple_of(j * chunk, chunk), chunk)] for g in range(n_s)], axis=0)
         hi = x.astype(jnp.bfloat16)
@@ -232,7 +228,7 @@
     both = gram[:total] + gram[total:]
     both = both + pltpu.roll(both, total, 1)
     for g in range(n_s):
-        part[g] = both[g * rows : (g + 1) * rows]
+        part[g] = pack(both[g * rows : (g + 1) * rows])
 
     def first_stage(d):
         peer = lax.rem(s + d, n_s)
@@ -244,12 +240,13 @@
         first_stage(d).start()
 
     lane = lax.broadcasted_iota(jnp.int32, (rows, 2 * total), 1)
+    lane = jnp.where(lane < total, lane, lane - total)
     first_k = jnp.zeros((rows, 2 * total), jnp.int32)
     last_k = jnp.zeros((rows, 2 * total), jnp.int32)
     for i in range(total):
         first_k = jnp.where(lane == i, vs[i], first_k)
         last_k = jnp.where(lane == i, ve[i], last_k)
-    count = (jnp.minimum(last_k, last) - jnp.maximum(first_k, first)).astype(f32)
+    count = pack((jnp.minimum(last_k, last) - jnp.maximum(first_k, first)).astype(f32))
 
     own = part[s]
     for d in range(1, n_s):
@@ -282,9 +279,27 @@
     full = r2[0]
     for d in range(1, n_t):
         full = full + r2[d]
-    cov[...] = (full / count)[:, :total]
+    full = full / count
+    cov[:half] = full[:, :total]
+    cov[half:] = pltpu.roll(full, total, 1)[:, :total]
     for d in range(1, n_t):
         second_stage(d).wait_send()
+
+
+FLUSHES = 4
+
+
+def flush(smooth, slope, cov, smooth_out, slope_out, cov_out, sems, cov_sem):
+    piece = smooth.shape[1] // FLUSHES
+    copies = [pltpu.make_async_copy(cov, cov_out, cov_sem)]
+    for i in range(FLUSHES):
+        span = pl.ds(i * piece, piece)
+        copies.append(pltpu.make_async_copy(smooth.at[:, span], smooth_out.at[:, span], sems.at[2 * i]))
+        copies.append(pltpu.make_async_copy(slope.at[:, span], slope_out.at[:, span], sems.at[2 * i + 1]))
+    for copy in copies:
+        copy.start()
+    for copy in copies:
+        copy.wait()
 
 
 def solution(mesh):
@@ -298,7 +313,7 @@
         sends = (n_s - 1) * (quarter // chunk)
         f32 = jnp.float32
         dma = pltpu.SemaphoreType.DMA
-        return pl.pallas_call(
+        kept = pl.pallas_call(
             functools.partial(kernel, n_s, n_t, rows, width, chunk),
             out_shape=(
                 jax.ShapeDtypeStruct((rows, width), f32),
@@ -316,17 +331,15 @@
                 pltpu.SMEM((total,), jnp.int32),
                 pltpu.VMEM((rows, width + 2 * LANE), f32),
                 pltpu.VMEM((2 * LANE, 2 * LANE), f32),
-                pltpu.VMEM((4, rows, LANE), f32),
-                pltpu.VMEM((6, rows, LANE), f32),
                 pltpu.VMEM((2, rows, LANE), jnp.int32),
                 pltpu.VMEM((rows, width), f32),
                 pltpu.VMEM((n_s, rows, quarter), f32),
                 pltpu.VMEM((2, rows, LANE), f32),
-                pltpu.VMEM((n_s, rows, 2 * total), f32),
-                pltpu.VMEM((n_s - 1, rows, 2 * total), f32),
-                pltpu.VMEM((rows, 2 * total), f32),
-                pltpu.VMEM((n_t, rows, 2 * total), f32),
-                dma,
+                pltpu.VMEM((n_s, rows // 2, 2 * total), f32),
+                pltpu.VMEM((n_s - 1, rows // 2, 2 * total), f32),
+                pltpu.VMEM((rows // 2, 2 * total), f32),
+                pltpu.VMEM((n_t, rows // 2, 2 * total), f32),
+                dma((n_s,)),
                 dma((2,)),
                 dma((2,)),
                 dma((2,)),
@@ -338,9 +351,17 @@
                 dma((n_t - 1,)),
             ],
             compiler_params=pltpu.CompilerParams(
-                collective_id=0, has_side_effects=True, vmem_limit_bytes=67043328 - 8 * rows * width - rows * width
+                collective_id=0, has_side_effects=True, vmem_limit_bytes=67043328 - 8 * rows * width - 12 * 1024 * 1024
             ),
         )(valid_start, valid_end, signal)
+        return pl.pallas_call(
+            flush,
+            out_shape=tuple(jax.ShapeDtypeStruct(v.shape, f32) for v in kept),
+            in_specs=[pl.BlockSpec(memory_space=pltpu.VMEM)] * 3,
+            out_specs=(pl.BlockSpec(memory_space=pltpu.HBM),) * 3,
+            scratch_shapes=[dma((2 * FLUSHES,)), dma],
+            compiler_params=pltpu.CompilerParams(vmem_limit_bytes=1024 * 1024),
+        )(*kept)
 
     in_specs = (P("series", "tm"), P(), P())
     out_specs = (P("series", "tm"), P("series", "tm"), P("series", None))

time: 45.9 us -> 41.3 us (0.90)
  local copies, waits for them, and re-layouts: 5.12 us -> 1.3 us
  Pallas kernels: 39.9 us -> 39.2 us
    unnamed x7 -> x4, local copies, waits for them, and re-layouts: 5.12 us -> 1.3 us
    pallas_call x1, Pallas kernels: 39.9 us -> 37.1 us  [shards(): pl.pallas_call(functools.partial(kernel, n_s, n_t, rows, width, chunk), o...]
    pallas_call x0 -> x1, Pallas kernels: none -> 2.09 us  [shards(): pl.pallas_call(flush, out_shape=tuple((jax.ShapeDtypeStruct(v.shape, f32)...]
where the time goes in v2:
time: 41.3 us; the launch traced here: 41.1 us
  Pallas kernels  39.2 us (95%)
  local copies, waits for them, and re-layouts  1.3 us (3%)
  between operations  0.65 us (2%)
    pallas_call x1, Pallas kernels, shards(): pl.pallas_call(functools.partial(kernel, n_s, n_t, rows, width, chunk), o...  37.1 us
    pallas_call x1, Pallas kernels, shards(): pl.pallas_call(flush, out_shape=tuple((jax.ShapeDtypeStruct(v.shape, f32)...  2.09 us
    unnamed x4, local copies, waits for them, and re-layouts  1.3 us

profile of v2, /device:TPU:0, one launch (start us, length us, event | category | flops | bytes accessed | tf_op | source)
XLA Modules:
  0.0 41.1 jit_solution(11989677796585257589)
XLA Ops:
  0.6 0.0 copy-start
  0.6 0.6 %copy-done = s32[64]{0:T(128)S(1)} copy-done((s32[64]{0:T(128)S(1)}, s32[64]{0:T(128)}, u32[]{:S(2)}) %copy-start) | copy-done | bytes 280
  1.3 0.0 copy-start.1
  1.3 0.7 %copy-done.1 = s32[64]{0:T(128)S(1)} copy-done((s32[64]{0:T(128)S(1)}, s32[64]{0:T(128)}, u32[]{:S(2)}) %copy-start.1) | copy-done | bytes 280
  1.9 37.1 %shard_map.58 = (f32[16,32768]{1,0:T(8,128)S(1)}, f32[16,32768]{1,0:T(8,128)S(1)}, f32[16,64]{1,0:T(8,128)S(1)}) custom-call(s32[64]{0:T(128)S(1)} %copy-done, s32[64]{0:T(128)S(1)} %copy-done.1, f32[16,32768]{1,0:T(8,128)} %sig_hbm.1), custom_call_target="tpu_custom_call" | custom-call | tf_op jit(solution)/shard_map/pallas_call | solution.py:316
  39.0 2.1 %shard_map.59 = (f32[16,32768]{1,0:T(8,128)}, f32[16,32768]{1,0:T(8,128)}, f32[16,64]{1,0:T(8,128)}) custom-call(f32[16,32768]{1,0:T(8,128)S(1)} %get-tuple-element.6.smooth, f32[16,32768]{1,0:T(8,128)S(1)} %get-tuple-element.7.slope, f32[16,64]{1,0:T(8,128)S(1)} %get-tuple-element.8.cov), custom_call_target="tpu_custom_call" | custom-call | tf_op jit(solution)/shard_map/pallas_call | solution.py:357
Async XLA Ops:
  0.6 0.7 %copy-start = (s32[64]{0:T(128)S(1)}, s32[64]{0:T(128)}, u32[]{:S(2)}) copy-start(s32[64]{0:T(128)} %vs_hbm.1) | copy-start | bytes 772
  1.3 0.7 %copy-start.1 = (s32[64]{0:T(128)S(1)}, s32[64]{0:T(128)}, u32[]{:S(2)}) copy-start(s32[64]{0:T(128)} %ve_hbm.1) | copy-start | bytes 772

commit v3 on v2

--- a/solution.py
+++ b/solution.py
@@ -25,9 +25,9 @@
 
 def kernel(
     n_s, n_t, rows, width, chunk,
-    vs_hbm, ve_hbm, sig_hbm,
+    bounds_hbm, sig_hbm,
     smooth, slope, cov,
-    vs, ve, ext, wts, ends, res, mixed, halo, part, r1, mine, r2,
+    bounds, ext, wts, ends, res, mixed, halo, part, r1, mine, r2,
     load_sem, bound_sem, halo_send, halo_recv, send_sem, recv_sem, s1_send, s1_recv, s2_send, s2_recv,
 ):
     s = lax.axis_index("series")
@@ -40,10 +40,8 @@
     tiles = chunk // LANE
     f32 = jnp.float32
 
-    starts = pltpu.make_async_copy(vs_hbm, vs, bound_sem.at[0])
-    stops = pltpu.make_async_copy(ve_hbm, ve, bound_sem.at[1])
-    starts.start()
-    stops.start()
+    limits = pltpu.make_async_copy(bounds_hbm, bounds, bound_sem)
+    limits.start()
     def offset(qi):
         if n_s == 4:
             odd = lax.rem(s, 2)
@@ -73,15 +71,14 @@
     ext[:, :LANE] = jnp.zeros((rows, LANE), f32)
     ext[:, LANE + width :] = jnp.zeros((rows, LANE), f32)
 
-    starts.wait()
-    stops.wait()
+    limits.wait()
     row = lax.broadcasted_iota(jnp.int32, (rows, LANE), 0)
     begin = t * width
     first = jnp.zeros((rows, LANE), jnp.int32)
     last = jnp.zeros((rows, LANE), jnp.int32)
     for i in range(rows):
-        first = jnp.where(row == i, vs[s * rows + i], first)
-        last = jnp.where(row == i, ve[s * rows + i], last)
+        first = jnp.where(row == i, bounds[0, s * rows + i], first)
+        last = jnp.where(row == i, bounds[1, s * rows + i], last)
     ends[0] = first - begin
     ends[1] = last - begin
 
@@ -244,8 +241,8 @@
     first_k = jnp.zeros((rows, 2 * total), jnp.int32)
     last_k = jnp.zeros((rows, 2 * total), jnp.int32)
     for i in range(total):
-        first_k = jnp.where(lane == i, vs[i], first_k)
-        last_k = jnp.where(lane == i, ve[i], last_k)
+        first_k = jnp.where(lane == i, bounds[0, i], first_k)
+        last_k = jnp.where(lane == i, bounds[1, i], last_k)
     count = pack((jnp.minimum(last_k, last) - jnp.maximum(first_k, first)).astype(f32))
 
     own = part[s]
@@ -323,12 +320,10 @@
             in_specs=[
                 pl.BlockSpec(memory_space=pltpu.HBM),
                 pl.BlockSpec(memory_space=pltpu.HBM),
-                pl.BlockSpec(memory_space=pltpu.HBM),
             ],
             out_specs=(pl.BlockSpec(memory_space=pltpu.VMEM),) * 3,
             scratch_shapes=[
-                pltpu.SMEM((total,), jnp.int32),
-                pltpu.SMEM((total,), jnp.int32),
+                pltpu.SMEM((2, total), jnp.int32),
                 pltpu.VMEM((rows, width + 2 * LANE), f32),
                 pltpu.VMEM((2 * LANE, 2 * LANE), f32),
                 pltpu.VMEM((2, rows, LANE), jnp.int32),
@@ -340,7 +335,7 @@
                 pltpu.VMEM((rows // 2, 2 * total), f32),
                 pltpu.VMEM((n_t, rows // 2, 2 * total), f32),
                 dma((n_s,)),
-                dma((2,)),
+                dma,
                 dma((2,)),
                 dma((2,)),
                 dma((sends,)),
@@ -353,7 +348,7 @@
             compiler_params=pltpu.CompilerParams(
                 collective_id=0, has_side_effects=True, vmem_limit_bytes=67043328 - 8 * rows * width - 12 * 1024 * 1024
             ),
-        )(valid_start, valid_end, signal)
+        )(jnp.stack([valid_start, valid_end]), signal)
         return pl.pallas_call(
             flush,
             out_shape=tuple(jax.ShapeDtypeStruct(v.shape, f32) for v in kept),

time: 41.3 us -> 40.7 us (0.985)
  local copies, waits for them, and re-layouts: 1.3 us -> 0 us
  other arithmetic: 0 us -> 0.68 us
    unnamed x4 -> x0, local copies, waits for them, and re-layouts: 1.3 us -> none
    another operation x0 -> x1, other arithmetic: none -> 0.68 us  [shards(): jnp.stack([valid_start, valid_end])]
where the time goes in v3:
time: 40.7 us; the launch traced here: 40.5 us
  Pallas kernels  39.2 us (96%)
  other arithmetic  0.68 us (2%)
  between operations  0.64 us (2%)
    pallas_call x1, Pallas kernels, shards(): pl.pallas_call(functools.partial(kernel, n_s, n_t, rows, width, chunk), o...  37.1 us
    pallas_call x1, Pallas kernels, shards(): pl.pallas_call(flush, out_shape=tuple((jax.ShapeDtypeStruct(v.shape, f32)...  2.09 us

profile of v3, /device:TPU:0, one launch (start us, length us, event | category | flops | bytes accessed | tf_op | source)
XLA Modules:
  0.0 40.5 jit_solution(8101620439161128931)
XLA Ops:
  0.6 0.7 %pad_add_fusion.bounds_hbm = s32[2,64]{1,0:T(2,128)S(1)} fusion(s32[1,64]{1,0:T(1,128)} %bitcast.2, s32[1,64]{1,0:T(1,128)} %bitcast.3), kind=kLoop, calls=%fused_computation | loop fusion | flops 128 | bytes 1024 | tf_op jit(solution)/shard_map/stack | solution.py:351
  1.3 37.1 %shard_map.58 = (f32[16,32768]{1,0:T(8,128)S(1)}, f32[16,32768]{1,0:T(8,128)S(1)}, f32[16,64]{1,0:T(8,128)S(1)}) custom-call(s32[2,64]{1,0:T(2,128)S(1)} %pad_add_fusion.bounds_hbm, f32[16,32768]{1,0:T(8,128)} %sig_hbm.1), custom_call_target="tpu_custom_call" | custom-call | tf_op jit(solution)/shard_map/pallas_call | solution.py:313
  38.5 2.1 %shard_map.59 = (f32[16,32768]{1,0:T(8,128)}, f32[16,32768]{1,0:T(8,128)}, f32[16,64]{1,0:T(8,128)}) custom-call(f32[16,32768]{1,0:T(8,128)S(1)} %get-tuple-element.6.smooth, f32[16,32768]{1,0:T(8,128)S(1)} %get-tuple-element.7.slope, f32[16,64]{1,0:T(8,128)S(1)} %get-tuple-element.8.cov), custom_call_target="tpu_custom_call" | custom-call | tf_op jit(solution)/shard_map/pallas_call | solution.py:352
